TPU v7x, 1024 devices: a whole 4x4x32 slice. The times are simulated.
1024 devices in a mesh: dp: 8 (over z_lo), seq: 32 (over z_hi, y, core), tensor: 4 (over x).
Axes of the slice: x: 4, y: 4, z: 32 (z_hi: 4, z_lo: 8; z = z_hi * 8 + z_lo), core: 2. Of those that a mesh axis runs over, the one named last changes fastest.
Arguments:
- q_self: bfloat16 [8, 4096, 4096], P('dp', 'seq', 'tensor'), may hold values from -162 to 162
- k_self: bfloat16 [8, 4096, 1024], P('dp', 'seq', 'tensor'), may hold values from -6 to 6
- v_self: bfloat16 [8, 4096, 1024], P('dp', 'seq', 'tensor'), may hold values from -6 to 6
- docs: int32 [8, 4096], P('dp', 'seq'), may hold values from 0 to 31, never falling along the last dimension, each value on 1 to 3072 neighbouring positions
- q_cross: bfloat16 [8, 4096, 4096], P('dp', 'seq', 'tensor'), may hold values from -162 to 162
- cotangent: bfloat16 [8, 4096, 4096], P('dp', 'seq', 'tensor'), may hold values from -6 to 6
- img_keys: bfloat16 [8, 1024, 1024], P('dp', 'seq', 'tensor'), may hold values from -6 to 6
- features: bfloat16 [8, 1024, 1280], P('dp', 'seq'), may hold values from -6 to 6
- w_value: bfloat16 [1280, 1024], P(None, 'tensor'), may hold values from -0.15625 to 0.15625
- tiles: int32 [8, 32], P('dp'), may hold values from 1 to 4
- cite: int32 [8, 32], P('dp'), may hold values from 0 to 31, each once within a row
Outputs:
- combined: bfloat16 [8, 4096, 4096], P('dp', 'seq', 'tensor')
- weight_grad: float32 [1280, 1024], P(('dp', 'seq'), 'tensor')
Inputs may be any that keep to these rules, and one draw needn't show every extreme that they name: `docs`: along each sample the document numbers never fall; every document 0 to 31 has one or more tokens. `cite`: each sample's row names every image exactly once.
All inputs are finite; a program needn't handle non-finite values.
Results may differ from a plain program's by a relative error of at most 0.029.
Values may be sent and summed in bfloat16 or wider, within the bound.
A program may use at most 64 MiB of HBM per device.

v0:
```python
import math

import jax
import jax.numpy as jnp
from jax import lax
from jax.sharding import Mesh
from jax.sharding import PartitionSpec as P

HD = 128
TILE_TOK = 8
SEQ = ("seq_0", "seq_1", "seq_2")
DP_SEQ = ("dp", "seq_0", "seq_1", "seq_2")


MASK_FILL = -1e30


def laid_out(blocks, dim):
    shape = list(blocks.shape[1:])
    shape[dim] *= blocks.shape[0]
    return jnp.moveaxis(blocks, 0, dim).reshape(shape)


def all_blocks(x, axes, sequence):
    blocks = x[None]
    for k in sequence:
        blocks = lax.all_gather(blocks, axes[k], axis=0, tiled=True)
    held = [lax.axis_size(axes[k]) for k in reversed(sequence)]
    blocks = blocks.reshape(*held, *x.shape)
    turned = sorted(range(len(sequence)), key=lambda place: sequence[len(sequence) - 1 - place])
    return blocks.transpose(*turned, *range(len(sequence), blocks.ndim)).reshape(-1, *x.shape)


def gathered_by_axis(x, axes, sequence, dim):
    return laid_out(all_blocks(x, axes, sequence), dim)


def sent_together(arrays, axis, dim, along):
    both = jnp.concatenate(arrays, axis=along)
    filled, at, gathered = (lax.all_gather(both, axis, axis=dim, tiled=True), 0, [])
    for a in arrays:
        gathered.append(lax.slice_in_dim(filled, at, at + a.shape[along], axis=along))
        at += a.shape[along]
    return tuple(gathered)


def in_blocks(x, dim, count):
    before, after = (x.shape[:dim], x.shape[dim + 1 :])
    return jnp.moveaxis(x.reshape(*before, count, -1, *after), dim, 0)


def sent_and_summed(x, axis, dim):
    blocks = in_blocks(x, dim, lax.axis_size(axis))
    arrived = lax.all_to_all(blocks, axis, split_axis=0, concat_axis=0, tiled=True)
    return arrived.astype(jnp.float32).sum(axis=0)


def absorb_block(
    running, queries, key_rows, value_rows, key_docs, key_pos, query_pos, my_docs, score_scale
):
    running_max, denominator, numerator = running
    kv_local = queries.shape[1]
    key_count = key_rows.shape[0]
    key_heads = key_rows.reshape(key_count, kv_local, HD)
    value_heads = value_rows.reshape(key_count, kv_local, HD)
    scores = (
        jnp.einsum("tgcd,sgd->gcts", queries, key_heads, preferred_element_type=jnp.float32)
        * score_scale
    )
    kept = (query_pos[:, None] >= key_pos[None, :]) & (my_docs[:, None] == key_docs[None, :])
    scores = jnp.where(kept, scores, MASK_FILL)
    new_max = jnp.maximum(running_max, jnp.max(scores, axis=-1))
    factor = jnp.exp(running_max - new_max)
    weights = jnp.where(kept, jnp.exp(scores - new_max[..., None]), 0.0)
    denominator = factor * denominator + jnp.sum(weights, axis=-1)
    numerator = factor[..., None] * numerator + jnp.einsum(
        "gcts,sgd->gctd",
        weights.astype(jnp.bfloat16),
        value_heads,
        preferred_element_type=jnp.float32,
    )
    return (new_max, denominator, numerator)


def on_device(
    q_self, k_self, v_self, docs, q_cross, cotangent, img_keys, features, w_value, tiles, cite
):
    tok_rows = q_self.shape[1]
    kv_local = k_self.shape[2] // HD
    heads_local = q_self.shape[2] // HD
    group_size = heads_local // kv_local
    score_scale = HD ** (-0.5)
    first_row = lax.axis_index(SEQ) * tok_rows
    last_row = first_row + tok_rows - 1
    query_pos = first_row + jnp.arange(tok_rows, dtype=jnp.int32)
    my_docs = docs[0]
    queries = q_self[0].reshape(tok_rows, kv_local, group_size, HD)
    start_state = (
        jnp.full((kv_local, group_size, tok_rows), MASK_FILL, jnp.float32),
        jnp.zeros((kv_local, group_size, tok_rows), jnp.float32),
        jnp.zeros((kv_local, group_size, tok_rows, HD), jnp.float32),
    )
    piece_keys = gathered_by_axis(k_self, SEQ, (0, 1, 2), 1)
    piece_values = gathered_by_axis(v_self, SEQ, (0, 1, 2), 1)
    piece_docs = gathered_by_axis(docs, SEQ, (0, 1, 2), 1)
    key_count = piece_keys.shape[1]
    block_rows = math.gcd(key_count, 512)
    block_count = key_count // block_rows
    key_blocks = piece_keys[0].reshape(block_count, block_rows, -1)
    value_blocks = piece_values[0].reshape(block_count, block_rows, -1)
    doc_blocks = piece_docs[0].reshape(block_count, block_rows)
    pos_blocks = jnp.arange(key_count, dtype=jnp.int32).reshape(block_count, block_rows)

    def absorb_step(state_now, block_item):
        key_part, value_part, doc_part, pos_part = block_item
        return (
            absorb_block(
                state_now,
                queries,
                key_part,
                value_part,
                doc_part,
                pos_part,
                query_pos,
                my_docs,
                score_scale,
            ),
            None,
        )

    def absorb_all(state_now):
        return lax.scan(absorb_step, state_now, (key_blocks, value_blocks, doc_blocks, pos_blocks))[
            0
        ]

    unused = (jnp.int32(0) > last_row) | (jnp.max(piece_docs) < my_docs[0])
    running_max, denominator, numerator = lax.cond(
        unused, lambda state_now: state_now, absorb_all, start_state
    )
    self_out = numerator / denominator[..., None]
    values_own = jnp.dot(features[0], w_value, preferred_element_type=jnp.float32).astype(
        jnp.bfloat16
    )
    image_keys, image_values = sent_together((img_keys[0], values_own), SEQ, 0, 1)
    key_count = image_keys.shape[0]
    slot_count = img_keys.shape[1]
    image_count = tiles.shape[1]
    doc_hit = my_docs[:, None] == jnp.arange(cite.shape[1], dtype=jnp.int32)[None, :]
    image_of = jnp.sum(jnp.where(doc_hit, cite[0][None, :], 0), axis=1)
    slot_ids = jnp.arange(key_count, dtype=jnp.int32)
    key_image = slot_ids // slot_count
    owner_hit = key_image[:, None] == jnp.arange(image_count, dtype=jnp.int32)[None, :]
    tile_limit = jnp.sum(jnp.where(owner_hit, tiles[0][None, :], 0), axis=1) * TILE_TOK
    cross_kept = (image_of[:, None] == key_image[None, :]) & (slot_ids % slot_count < tile_limit)[
        None, :
    ]
    cross_q = q_cross[0].reshape(tok_rows, kv_local, group_size, HD)
    cross_scores = (
        jnp.einsum(
            "tgcd,sgd->gcts",
            cross_q,
            image_keys.reshape(key_count, kv_local, HD),
            preferred_element_type=jnp.float32,
        )
        * score_scale
    )
    cross_scores = jnp.where(cross_kept, cross_scores, MASK_FILL)
    cross_exp = jnp.where(
        cross_kept, jnp.exp(cross_scores - jnp.max(cross_scores, axis=-1, keepdims=True)), 0.0
    )
    cross_weights = (cross_exp / jnp.sum(cross_exp, axis=-1, keepdims=True)).astype(jnp.bfloat16)
    cross_out = jnp.einsum(
        "gcts,sgd->gctd",
        cross_weights,
        image_values.reshape(key_count, kv_local, HD),
        preferred_element_type=jnp.float32,
    )
    merged = (
        (self_out + cross_out)
        .astype(jnp.bfloat16)
        .transpose(2, 0, 1, 3)
        .reshape(1, tok_rows, heads_local * HD)
    )
    cot_rows = cotangent[0].reshape(tok_rows, kv_local, group_size, HD)
    grad_terms = jnp.einsum(
        "gcts,tgcd->sgd", cross_weights, cot_rows, preferred_element_type=jnp.float32
    ).reshape(key_count, kv_local * HD)
    value_grad = lax.psum_scatter(
        grad_terms.astype(jnp.bfloat16), SEQ, scatter_dimension=0, tiled=True
    )
    own_features = features[0]
    summed_samples = sent_and_summed(
        lax.dot_general(
            own_features, value_grad, (((0,), (0,)), ((), ())), preferred_element_type=jnp.float32
        ).astype(jnp.bfloat16),
        "dp",
        0,
    )
    weight_grad = sent_and_summed(summed_samples.astype(jnp.bfloat16), SEQ, 0)
    return (merged, weight_grad)


def solution(mesh):
    split = Mesh(
        mesh.devices.reshape(mesh.shape["dp"], 4, 4, 2, mesh.shape["tensor"]),
        ("dp", "seq_0", "seq_1", "seq_2", "tensor"),
    )
    placed = (
        P("dp", SEQ, "tensor"),
        P("dp", SEQ, "tensor"),
        P("dp", SEQ, "tensor"),
        P("dp", SEQ),
        P("dp", SEQ, "tensor"),
        P("dp", SEQ, "tensor"),
        P("dp", SEQ, "tensor"),
        P("dp", SEQ, None),
        P(None, "tensor"),
        P("dp", None),
        P("dp", None),
    )
    return jax.shard_map(
        on_device,
        mesh=split,
        in_specs=placed,
        out_specs=(P("dp", SEQ, "tensor"), P(DP_SEQ, "tensor")),
        check_vma=False,
    )
```

profile of v0, /device:TPU:1, one launch (start us, length us, event | category | flops | bytes accessed | tf_op | source)
XLA Modules:
  0.0 467.5 jit_solution(15988625913352739775)
XLA Ops:
  8.1 1.0 copy-done
  9.1 1.1 convolution_convert_fusion.1
  10.2 1.4 pad_maximum_fusion
  11.6 1.1 reshape_squeeze.11
  12.7 1.1 copy.108
  13.9 0.8 select_reduce_fusion.1
  14.6 0.7 select_reduce_fusion
  15.7 121.9 %all-gather.17.cloned.1.call-done = bf16[1024,512]{1,0:T(8,128)(2,1)} async-done(((bf16[32,512]{1,0:T(8,128)(2,1)}), bf16[1024,512]{1,0:T(8,128)(2,1)}) %all-gather.17.cloned.1.call-update) | async-done | bytes 1048592 | tf_op jit(solution)/shard_map/all_gather | solution.py:40
  137.7 1.3 fusion.35
  139.8 2.1 fusion.36
  142.2 1.3 copy-done.1
  143.5 0.8 fusion.18
  144.4 1.0 copy.113
  145.5 34.7 %all-gather.6 = bf16[4,128,256]{2,1,0:T(8,128)(2,1)} all-gather(bf16[1,128,256]{2,1,0:T(8,128)(2,1)S(1)} %copy-done.5), channel_id=8, replica_groups=mesh['dp'=8,'seq_0'=4,'seq_1'=4,'seq_2'=2,'tensor'=4] {'seq_0'}, dimensions={0}, use_global_device_ids=true | all-gather | bytes 327680 | tf_op jit(solution)/shard_map/all_gather | solution.py:27
  180.2 31.6 %all-gather.3 = bf16[4,128,256]{2,1,0:T(8,128)(2,1)} all-gather(bf16[1,128,256]{2,1,0:T(8,128)(2,1)S(1)} %copy-done.6), channel_id=5, replica_groups=mesh['dp'=8,'seq_0'=4,'seq_1'=4,'seq_2'=2,'tensor'=4] {'seq_0'}, dimensions={0}, use_global_device_ids=true | all-gather | bytes 327680 | tf_op jit(solution)/shard_map/all_gather | solution.py:27
  211.8 79.9 %reduce-scatter.4.cloned.1.call-done = bf16[32,256]{1,0:T(8,128)(2,1)} async-done(((bf16[1024,256]{1,0:T(8,128)(2,1)}), bf16[32,256]{1,0:T(8,128)(2,1)}) %reduce-scatter.4.cloned.1.call-update) | async-done | bytes 16400
  291.7 1.1 fusion.14
  292.8 1.1 copy.95
  293.9 6.7 %all-to-all-start = ((bf16[8,160,256]{2,1,0:T(8,128)(2,1)}), bf16[8,160,256]{2,1,0:T(8,128)(2,1)S(1)}, u32[]{:S(2)}, u32[]{:S(2)}) async-start(bf16[8,160,256]{2,1,0:T(8,128)(2,1)} %bitcast.31), calls=%async_computation | async-start | bytes 1310720 | tf_op jit(solution)/shard_map/all_to_all | solution.py:54
  301.9 22.8 %all-to-all-done = bf16[8,160,256]{2,1,0:T(8,128)(2,1)S(1)} async-done(((bf16[8,160,256]{2,1,0:T(8,128)(2,1)}), bf16[8,160,256]{2,1,0:T(8,128)(2,1)S(1)}, u32[]{:S(2)}, u32[]{:S(2)}) %all-to-all-start) | async-done | bytes 655392 | tf_op jit(solution)/shard_map/all_to_all | solution.py:54
  325.5 25.2 %all-to-all-start.1 = ((bf16[32,5,256]{2,1,0:T(8,128)(2,1)}), bf16[32,5,256]{2,1,0:T(8,128)(2,1)S(1)}, u32[]{:S(2)}, u32[]{:S(2)}) async-start(bf16[32,5,256]{2,1,0:T(8,128)(2,1)} %reshape.103), calls=%async_computation.1 | async-start | bytes 262144 | tf_op jit(solution)/shard_map/all_to_all | solution.py:54
  350.7 24.0 %all-gather.9 = s32[4,1,128]{2,1,0:T(1,128)S(1)} all-gather(s32[1,1,128]{2,1,0:T(1,128)S(1)} %bitcast.131), channel_id=2, replica_groups=mesh['dp'=8,'seq_0'=4,'seq_1'=4,'seq_2'=2,'tensor'=4] {'seq_0'}, dimensions={0}, use_global_device_ids=true | all-gather | bytes 2560 | tf_op jit(solution)/shard_map/all_gather | solution.py:27
  374.7 8.3 %all-gather.10 = s32[4,4,128]{2,1,0:T(4,128)S(1)} all-gather(s32[1,4,128]{2,1,0:T(4,128)S(1)} %bitcast.135), channel_id=3, replica_groups=mesh['dp'=8,'seq_0'=4,'seq_1'=4,'seq_2'=2,'tensor'=4] {'seq_1'}, dimensions={0}, use_global_device_ids=true | all-gather | bytes 10240 | tf_op jit(solution)/shard_map/all_gather | solution.py:27
  383.0 7.8 %all-gather.2 = s32[32,128]{1,0:T(8,128)S(1)} all-gather(s32[16,128]{1,0:T(8,128)S(1)} %bitcast.129), channel_id=4, replica_groups=mesh['dp'=8,'seq_0'=4,'seq_1'=4,'seq_2'=2,'tensor'=4] {'seq_2'}, dimensions={0}, use_global_device_ids=true | all-gather | bytes 24576 | tf_op jit(solution)/shard_map/all_gather | solution.py:27
  392.1 1.0 copy.107
  393.2 61.7 %conditional.1 = (f32[2,4,128]{2,1,0:T(4,128)S(1)}, f32[2,4,128,128]{3,2,1,0:T(8,128)}) conditional(s32[]{:T(128)} %convert_element_type.35, (bf16[4,4,2,1,128,256]{5,4,0,1,2,3:T(8,128)(2,1)}, bf16[4,4,2,1,128,256]{5,4,0,1,2,3:T(8,128)(2,1)}, s32[4,4,2,1,128]{4,0,1,2,3:T(4,128)S(1)}, s32[8,512]{1,0:T(8,128)S(1)}, s32[8,512]{1,0:T(8,128)S(1)}, ...), branch_computations={%region_1.6_spmd, %region_6.7_spmd} | conditional | flops 275854464 | bytes 28506416 | solution.py:137
  393.2 3.3 copy.84
  396.5 1.5 copy.85
  398.2 0.9 copy.82
  399.7 55.2 %while.18 = (s32[]{:T(128)}, f32[2,4,128]{2,1,0:T(4,128)S(1)}, f32[2,4,128]{2,1,0:T(4,128)S(1)}, f32[2,4,128,128]{3,2,1,0:T(8,128)}, s32[128]{0:T(128)S(1)}, /*i...) while((s32[]{:T(128)}, f32[2,4,128]{2,1,0:T(4,128)S(1)}, ...), condition=%wide.region_5.5_spmd.clone, body=%wide.region_2.4_spmd.clone.sunk | while | flops 275846144 | bytes 10564753 | solution.py:132
  399.7 0.7 constant_dynamic-slice_fusion.6
  400.6 1.1 constant_dynamic-slice_fusion.7
  401.9 1.5 fusion.57
  404.1 1.6 convolution_add_fusion.3
  405.7 0.7 constant_dynamic-slice_fusion.6
  406.6 1.1 constant_dynamic-slice_fusion.7
  407.9 1.5 fusion.57
  410.1 2.7 convolution_add_fusion.3
  412.7 0.7 constant_dynamic-slice_fusion.6
  413.7 1.1 constant_dynamic-slice_fusion.7
  414.9 1.5 fusion.57
  417.1 2.7 convolution_add_fusion.3
  419.8 0.7 constant_dynamic-slice_fusion.6
  420.7 1.1 constant_dynamic-slice_fusion.7
  421.9 1.5 fusion.57
  424.1 2.7 convolution_add_fusion.3
  426.8 0.7 constant_dynamic-slice_fusion.6
  427.7 1.1 constant_dynamic-slice_fusion.7
  428.9 1.5 fusion.57
  431.1 2.7 convolution_add_fusion.3
  433.8 0.7 constant_dynamic-slice_fusion.6
  434.8 1.1 constant_dynamic-slice_fusion.7
  436.0 1.5 fusion.57
  438.2 2.7 convolution_add_fusion.3
  440.9 0.7 constant_dynamic-slice_fusion.6
  441.8 1.1 constant_dynamic-slice_fusion.7
  443.0 1.5 fusion.57
  445.2 2.7 convolution_add_fusion.3
  448.8 1.1 constant_dynamic-slice_fusion.7
  450.0 1.5 fusion.57
  452.2 2.7 convolution_add_fusion.3
  454.9 1.2 copy.88
  456.2 2.3 fusion.19
  458.4 0.9 copy.96
  (109 shorter events, 14.9 us)
Async XLA Ops:
  8.0 1.1 copy-start
  8.0 129.6 %all-gather.17.cloned.1.call-start = ((), (), s32[]{:S(2)}) async-start(), calls=%async_computation.3 | async-start | bytes 1081344 | tf_op jit(solution)/shard_map/all_gather | solution.py:40
  11.6 280.1 %reduce-scatter.4.cloned.1.call-start = ((), (), s32[]{:S(2)}) async-start(), calls=%async_computation.8 | async-start | bytes 540672
  142.2 1.3 copy-start.1
  143.5 1.9 copy-start.5
  143.5 36.7 %copy-start.6 = (bf16[1,128,256]{2,1,0:T(8,128)(2,1)S(1)}, bf16[1,128,256]{2,1,0:T(8,128)(2,1)}, u32[]{:S(2)}) copy-start(bf16[1,128,256]{2,1,0:T(8,128)(2,1)} %param.16) | copy-start | bytes 196612
  144.4 147.3 %copy-start.3 = (bf16[1,32,1280]{2,1,0:T(8,128)(2,1)S(1)}, bf16[1,32,1280]{2,1,0:T(8,128)(2,1)}, u32[]{:S(2)}) copy-start(bf16[1,32,1280]{2,1,0:T(8,128)(2,1)} %param.22) | copy-start | bytes 245764
  145.4 155.2 %all-gather.23.cloned.1.call-start = ((), (), s32[]{:S(2)}) async-start(), calls=%async_computation.6 | async-start | bytes 1310720 | tf_op jit(solution)/shard_map/all_gather | solution.py:27
  180.2 121.0 %all-gather.19.cloned.1.call-start = ((), (), s32[]{:S(2)}) async-start(), calls=%async_computation.4 | async-start | bytes 1310720 | tf_op jit(solution)/shard_map/all_gather | solution.py:27
  293.9 56.8 %copy-start.7 = (s32[1,128]{1,0:T(1,128)S(1)}, s32[1,128]{1,0:T(1,128)}, u32[]{:S(2)}) copy-start(s32[1,128]{1,0:T(1,128)} %param.18) | copy-start | bytes 1540
  293.9 30.8 %all-to-all-start = ((bf16[8,160,256]{2,1,0:T(8,128)(2,1)}), bf16[8,160,256]{2,1,0:T(8,128)(2,1)S(1)}, u32[]{:S(2)}, u32[]{:S(2)}) async-start(bf16[8,160,256]{2,1,0:T(8,128)(2,1)} %bitcast.31), calls=%async_computation | async-start | bytes 1310720 | tf_op jit(solution)/shard_map/all_to_all | solution.py:54
  300.5 92.6 %all-gather.25.cloned.1.call-start = ((), (), s32[]{:S(2)}) async-start(), calls=%async_computation.7 | async-start | bytes 3145728 | tf_op jit(solution)/shard_map/all_gather | solution.py:27
  300.6 92.6 %copy-start.4 = (bf16[1,128,1024]{2,1,0:T(8,128)(2,1)S(1)}, bf16[1,128,1024]{2,1,0:T(8,128)(2,1)}, u32[]{:S(2)}) copy-start(bf16[1,128,1024]{2,1,0:T(8,128)(2,1)} %param.15) | copy-start | bytes 786436
  301.1 92.0 %all-gather.21.cloned.1.call-start = ((), (), s32[]{:S(2)}) async-start(), calls=%async_computation.5 | async-start | bytes 3145728 | tf_op jit(solution)/shard_map/all_gather | solution.py:27
  325.5 133.8 %all-to-all-start.1 = ((bf16[32,5,256]{2,1,0:T(8,128)(2,1)}), bf16[32,5,256]{2,1,0:T(8,128)(2,1)S(1)}, u32[]{:S(2)}, u32[]{:S(2)}) async-start(bf16[32,5,256]{2,1,0:T(8,128)(2,1)} %reshape.103), calls=%async_computation.1 | async-start | bytes 262144 | tf_op jit(solution)/shard_map/all_to_all | solution.py:54
  393.2 3.3 copy-start.2
Sparse Core Ops, SparseCore 0:
  13.7 123.9 all-gather.16
  145.5 146.1 reduce-scatter.3
Sparse Core Ops, SparseCore 1:
  180.2 28.3 all-gather.22
  211.9 41.4 all-gather.18
  303.7 29.2 all-gather.24
  335.7 32.6 all-gather.20
where the time goes:
time: 469 us; the launch traced here: 468 us
  waiting for transfers between devices  226 us (48%)
  blocking collectives  106 us (23%)
  matrix products  38.2 us (8%)
  local copies, waits for them, and re-layouts  35.1 us (7%)
  starting transfers between devices  32.1 us (7%)
  between operations  16.6 us (4%)
  other arithmetic  13 us (3%)
    all_gather x1, waiting for transfers between devices, sent_together(): lax.all_gather(both, axis, axis=dim, tiled=True)  122 us
    all_gather x5, blocking collectives, all_blocks(): blocks = lax.all_gather(blocks, axes[k], axis=0, tiled=True)  106 us
    unnamed x7, waiting for transfers between devices  81.1 us
    all_to_all x2, starting transfers between devices, sent_and_summed(): lax.all_to_all(blocks, axis, split_axis=0, concat_axis=0, tiled=True)  31.9 us
    all_to_all x2, waiting for transfers between devices, sent_and_summed(): lax.all_to_all(blocks, axis, split_axis=0, concat_axis=0, tiled=True)  22.8 us
    dot_general x8, matrix products, absorb_block(): jnp.einsum('gcts,sgd->gctd', weights.astype(jnp.bfloat16), value_heads, p...  20.3 us
    dynamic_slice x32, local copies, waits for them, and re-layouts, absorb_all(): lax.scan(absorb_step, state_now, (key_blocks, value_blocks, doc_blocks, p...  16.6 us
    dot_general x8, matrix products, absorb_block(): jnp.einsum('tgcd,sgd->gcts', queries, key_heads, preferred_element_type=j...  11.9 us
  transfers between devices with their start and end apart: 8, of which 3 were waited for; matrix products, arithmetic and copies ran while one was open for 16% of the time, Pallas kernels for 0%

commit v1 on v0

v1 whole, which is shorter than its diff:
```python
import functools
import math

import jax
import jax.numpy as jnp
from jax import lax
from jax.experimental import pallas as pl
from jax.experimental.pallas import tpu as pltpu
from jax.sharding import Mesh
from jax.sharding import PartitionSpec as P

HD = 128
TILE_TOK = 8
IMG_TOK = 32
SEQ = ("seq_0", "seq_1", "seq_2")
DP_SEQ = ("dp", "seq_0", "seq_1", "seq_2")
NEG = -1e30
MESH = pl.DeviceIdType.MESH
SCORE = HD**-0.5 * math.log2(math.e)

OFF = (0, 3, 1, 2)
DOC, KEY, VAL = 0, 1, 2


def kernel(
    q_hbm, k_hbm, v_hbm, docs_hbm, qx_hbm, ct_hbm, ik_hbm, f_hbm, w_hbm, tiles_ref, cite_ref,
    out_ref, wg_ref,
    q, qx, ct, feat, w,
    kv, im, dg, fs, gf, gs, gr, zs, zr, vga, fw, fr,
    m_s, l_s, acc, xc, qd, lo, hi, vacc,
    lsem,
    zs_d, zr_d, zs_i, zr_i, zs_k, zr_k,
    ys_d, yr_d, ys_i, yr_i, ys_k, yr_k,
    cs, cr, fss, fsr, gss, gsr, rss, rsr, vss, vsr, wss, wsr,
):
    b = lax.axis_index("dp")
    h = lax.axis_index("seq_0")
    y = lax.axis_index("seq_1")
    c = lax.axis_index("seq_2")
    yc = y * 2 + c
    own = h * 8 + yc
    pz = h * 8 + b
    up, down, far = (h + 1) % 4, (h + 3) % 4, (h + 2) % 4
    right, left, across = (y + 1) % 4, (y + 3) % 4, (y + 2) % 4
    chunk = (h, down, up, far)
    sends = []

    def remote(src, dst, ss, rs, **where):
        return pltpu.make_async_remote_copy(
            src_ref=src, dst_ref=dst, send_sem=ss, recv_sem=rs, device_id=where, device_id_type=MESH
        )

    def send(src, dst, ss, rs, **where):
        copy = remote(src, dst, ss, rs, **where)
        copy.start()
        sends.append(copy)

    def arrive(dst, ss, rs):
        remote(dst, dst, ss, rs, seq_2=1 - c).wait_recv()

    def yc_of(delta):
        other = (yc + delta) % 8
        return other // 2, other % 2

    def z_of(delta):
        other = (pz + delta) % 32
        return other // 8, other % 8

    local = []

    def fetch(src, dst):
        copy = pltpu.make_async_copy(src, dst, lsem.at[len(local)])
        copy.start()
        local.append(copy)
        return copy

    got_f = fetch(f_hbm.at[0], feat)
    got_w = fetch(w_hbm, w)
    first = [
        fetch(docs_hbm, dg.at[c, h, y]),
        fetch(ik_hbm.at[0], im.at[c, h, y, 0]),
        fetch(k_hbm.at[0], kv.at[c, h, y, 0]),
        fetch(v_hbm.at[0], kv.at[c, h, y, 1]),
    ]
    rest = [fetch(q_hbm.at[0], q), fetch(qx_hbm.at[0], qx), fetch(ct_hbm.at[0], ct)]

    barrier = pltpu.get_barrier_semaphore()
    for delta in (16, *range(1, 16), *range(17, 32)):
        hh, bb = z_of(delta)
        pl.semaphore_signal(barrier, inc=1, device_id={"seq_0": hh, "dp": bb}, device_id_type=MESH)
    for delta in range(1, 8):
        yy, cc = yc_of(delta)
        pl.semaphore_signal(barrier, inc=1, device_id={"seq_1": yy, "seq_2": cc}, device_id_type=MESH)

    got_f.wait()
    got_w.wait()
    im[c, h, y, 1] = jnp.dot(feat[...], w[...], preferred_element_type=jnp.float32).astype(jnp.bfloat16)

    col = lax.broadcasted_iota(jnp.int32, (1, 256), 1)
    wanted = jnp.where(col % 8 < 5, (col // 8) * 40 + col % 8, -1000)
    vis_at = lax.broadcasted_iota(jnp.int32, (1280, 256), 0)

    def pick(partner, _):
        chosen = jnp.where(vis_at == wanted + partner * 5, 1.0, 0.0).astype(jnp.bfloat16)
        fs[partner] = jnp.dot(feat[...], chosen, preferred_element_type=jnp.float32).astype(jnp.bfloat16)
        return 0

    lax.fori_loop(0, 8, pick, 0)
    gf[yc] = fs[yc]

    m_s[...] = jnp.full_like(m_s, NEG)
    l_s[...] = jnp.zeros_like(l_s)
    acc[...] = jnp.zeros_like(acc)
    xc[...] = jnp.zeros_like(xc)

    for copy in first:
        copy.wait()
    my_docs = jnp.broadcast_to(dg[c, h, y].astype(jnp.float32), (128, 128)).T
    qd[...] = my_docs
    number = lax.broadcasted_iota(jnp.int32, (128, 32), 1).astype(jnp.float32)
    cites = jnp.broadcast_to(cite_ref[...].astype(jnp.float32), (128, 32))
    counts = jnp.broadcast_to(tiles_ref[...].astype(jnp.float32), (128, 32))
    image = jnp.sum(jnp.where(number == my_docs[:, :32], cites, 0.0), axis=1, keepdims=True)
    tile_count = jnp.sum(jnp.where(number == image, counts, 0.0), axis=1, keepdims=True)
    lo[...] = jnp.broadcast_to(image * IMG_TOK, (128, 128))
    hi[...] = jnp.broadcast_to(image * IMG_TOK + tile_count * TILE_TOK, (128, 128))

    pl.semaphore_wait(barrier, 38)

    def doc(hc, yy):
        return dg.at[c, hc, yy]

    def img(hc, yy):
        return im.at[c, hc, yy]

    def item(hc, yy, which):
        return kv.at[c, hc, yy, which]

    def half(hc, which, part):
        return kv.at[c, hc, y, which, pl.ds(part * 64, 64)]

    def z_half(which, part, way):
        n = which * 2 + part
        where = up if way == 0 else down
        send(half(h, which, part), half(h, which, part), zs_k.at[way, n], zr_k.at[way, n], seq_0=where)

    def z_half_in(which, part, way):
        n = which * 2 + part
        hc = down if way == 0 else up
        arrive(half(hc, which, part), zs_k.at[way, n], zr_k.at[way, n])

    def y_first_small(r):
        hc = chunk[r]
        for way, where in ((0, right), (1, left)):
            send(doc(hc, y), doc(hc, y), ys_d.at[r, way], yr_d.at[r, way], seq_1=where)
            send(img(hc, y), img(hc, y), ys_i.at[r, way], yr_i.at[r, way], seq_1=where)

    def y_second_small(r):
        hc = chunk[r]
        arrive(doc(hc, left), ys_d.at[r, 0], yr_d.at[r, 0])
        send(doc(hc, left), doc(hc, left), ys_d.at[r, 2], yr_d.at[r, 2], seq_1=right)
        arrive(img(hc, left), ys_i.at[r, 0], yr_i.at[r, 0])
        send(img(hc, left).at[0], img(hc, left).at[0], ys_i.at[r, 2], yr_i.at[r, 2], seq_1=right)
        arrive(doc(hc, right), ys_d.at[r, 1], yr_d.at[r, 1])
        arrive(img(hc, right), ys_i.at[r, 1], yr_i.at[r, 1])
        send(img(hc, right).at[1], img(hc, right).at[1], ys_i.at[r, 3], yr_i.at[r, 3], seq_1=left)

    def core_small(r):
        hc = chunk[r]
        arrive(doc(hc, across), ys_d.at[r, 2], yr_d.at[r, 2])
        send(dg.at[c, hc], dg.at[c, hc], cs.at[DOC, r], cr.at[DOC, r], seq_2=1 - c)
        arrive(img(hc, across).at[0], ys_i.at[r, 2], yr_i.at[r, 2])
        arrive(img(hc, across).at[1], ys_i.at[r, 3], yr_i.at[r, 3])
        send(im.at[c, hc], im.at[c, hc], cs.at[KEY, r], cr.at[KEY, r], seq_2=1 - c)

    def core_small_in(r):
        hc = chunk[r]
        arrive(dg.at[1 - c, hc], cs.at[DOC, r], cr.at[DOC, r])
        arrive(im.at[1 - c, hc], cs.at[KEY, r], cr.at[KEY, r])

    def y_first(r, which):
        hc = chunk[r]
        for way, where in ((0, right), (1, left)):
            send(item(hc, y, which), item(hc, y, which), ys_k.at[r, which, way], yr_k.at[r, which, way], seq_1=where)

    def y_second(r, which):
        hc = chunk[r]
        if which == 0:
            arrive(item(hc, left, 0), ys_k.at[r, 0, 0], yr_k.at[r, 0, 0])
            send(item(hc, left, 0), item(hc, left, 0), ys_k.at[r, 0, 2], yr_k.at[r, 0, 2], seq_1=right)
            arrive(item(hc, right, 0), ys_k.at[r, 0, 1], yr_k.at[r, 0, 1])
        else:
            arrive(item(hc, right, 1), ys_k.at[r, 1, 1], yr_k.at[r, 1, 1])
            send(item(hc, right, 1), item(hc, right, 1), ys_k.at[r, 1, 2], yr_k.at[r, 1, 2], seq_1=left)
            arrive(item(hc, left, 1), ys_k.at[r, 1, 0], yr_k.at[r, 1, 0])

    def core(r):
        hc = chunk[r]
        arrive(item(hc, across, 0), ys_k.at[r, 0, 2], yr_k.at[r, 0, 2])
        arrive(item(hc, across, 1), ys_k.at[r, 1, 2], yr_k.at[r, 1, 2])
        send(kv.at[c, hc], kv.at[c, hc], cs.at[VAL, r], cr.at[VAL, r], seq_2=1 - c)

    def core_in(r):
        hc = chunk[r]
        arrive(kv.at[1 - c, hc], cs.at[VAL, r], cr.at[VAL, r])

    def stacked(ref, g):
        return jnp.concatenate(
            [ref[:, pl.ds(pl.multiple_of(g * 512 + i * 128, 128), 128)] for i in range(4)], axis=0
        )

    def lanes(g):
        return pl.ds(pl.multiple_of(g * 128, 128), 128)

    def cross(r):
        hc = chunk[r]

        def one(g, _):
            keys = jnp.concatenate([im[i, hc, :, 0, :, lanes(g)].reshape(128, 128) for i in (0, 1)], axis=0)
            values = jnp.concatenate([im[i, hc, :, 1, :, lanes(g)].reshape(128, 128) for i in (0, 1)], axis=0)
            s = lax.dot_general(
                stacked(qx, g), keys, (((1,), (1,)), ((), ())), preferred_element_type=jnp.float32
            )
            at = lax.broadcasted_iota(jnp.int32, (1, 256), 1)
            slot = (((hc * 4 + (at % 128) // 32) * 2 + at // 128) * 32 + at % 32).astype(jnp.float32)
            bias = jnp.where((slot >= lo[:, :1]) & (slot < hi[:, :1]), 0.0, NEG)
            s = (s.reshape(4, 128, 256) * SCORE + bias[None]).reshape(512, 256)
            top = jnp.max(s, axis=1, keepdims=True)
            e = jnp.exp2(s - top)
            total = jnp.sum(e, axis=1, keepdims=True)
            weights = (e * jnp.where(top > 0.5 * NEG, 1.0 / total, 0.0)).astype(jnp.bfloat16)
            xc[g] += jnp.dot(weights, values, preferred_element_type=jnp.float32)
            grad = lax.dot_general(
                weights, stacked(ct, g), (((0,), (0,)), ((), ())), preferred_element_type=jnp.float32
            ).astype(jnp.bfloat16)
            for i in (0, 1):
                gs[r, i, :, :, lanes(g)] = grad[i * 128 : (i + 1) * 128].reshape(4, 32, 128)
            return 0

        lax.fori_loop(0, 2, one, 0)

    def attend(r):
        hc = chunk[r]

        def one(n, _):
            g, half_at = n // 2, n % 2
            keys = kv[half_at, hc, :, 0, :, lanes(g)].reshape(512, 128)
            values = kv[half_at, hc, :, 1, :, lanes(g)].reshape(512, 128)
            s = lax.dot_general(
                stacked(q, g), keys, (((1,), (1,)), ((), ())), preferred_element_type=jnp.float32
            )
            key_doc = jnp.concatenate([dg[half_at, hc, i] for i in range(4)], axis=1).astype(jnp.float32)
            at = lax.broadcasted_iota(jnp.int32, (128, 512), 1)
            key_pos = ((hc * 4 + at // 128) * 2 + half_at) * 128 + at % 128
            row_pos = own * 128 + lax.broadcasted_iota(jnp.int32, (128, 512), 0)
            bias = jnp.where((key_doc == qd[:, :1]) & (key_pos <= row_pos), 0.0, NEG)
            s = (s.reshape(4, 128, 512) * SCORE + bias[None]).reshape(512, 512)
            old = m_s[g][:, :1]
            top = jnp.maximum(old, jnp.max(s, axis=1, keepdims=True))
            e = jnp.exp2(s - top)
            fade = jnp.exp2(old - top)
            m_s[g] = jnp.broadcast_to(top, (512, 128))
            l_s[g] = l_s[g] * fade + jnp.broadcast_to(jnp.sum(e, axis=1, keepdims=True), (512, 128))
            acc[g] = acc[g] * fade + jnp.dot(e.astype(jnp.bfloat16), values, preferred_element_type=jnp.float32)
            return 0

        lax.fori_loop(0, 4, one, 0)

    def grad_out(r):
        for delta in range(1, 8):
            yy, cc = yc_of(delta)
            send(gs.at[r, cc, yy], gr.at[r, delta], gss.at[r, delta], gsr.at[r, delta], seq_1=yy, seq_2=cc)

    def grad_in(r):
        total = gs[r, c, y].astype(jnp.float32)
        for delta in range(1, 8):
            arrive(gr.at[r, delta], gss.at[r, delta], gsr.at[r, delta])
        for delta in range(1, 8):
            total += gr[r, delta].astype(jnp.float32)
        return total

    def owner_out(r):
        zs[r] = grad_in(r).astype(jnp.bfloat16)
        send(zs.at[r], zr.at[r], rss.at[r], rsr.at[r], seq_0=chunk[r])

    for way, where in ((0, up), (1, down)):
        send(doc(h, y), doc(h, y), zs_d.at[way], zr_d.at[way], seq_0=where)
        send(img(h, y), img(h, y), zs_i.at[way], zr_i.at[way], seq_0=where)
    z_half(0, 0, 0)
    z_half(1, 0, 1)
    y_first_small(0)
    for delta in range(1, 8):
        yy, cc = yc_of(delta)
        send(fs.at[yy * 2 + cc], gf.at[yc], fss.at[delta], fsr.at[delta], seq_1=yy, seq_2=cc)
    y_first(0, 0)
    y_first(0, 1)
    for copy in rest:
        copy.wait()

    y_second_small(0)
    core_small(0)
    y_second(0, 0)
    y_second(0, 1)
    core_small_in(0)
    cross(0)
    grad_out(0)
    core(0)

    arrive(doc(down, y), zs_d.at[0], zr_d.at[0])
    send(doc(down, y), doc(down, y), zs_d.at[2], zr_d.at[2], seq_0=up)
    arrive(img(down, y), zs_i.at[0], zr_i.at[0])
    send(img(down, y).at[0], img(down, y).at[0], zs_i.at[2], zr_i.at[2], seq_0=up)
    arrive(doc(up, y), zs_d.at[1], zr_d.at[1])
    arrive(img(up, y), zs_i.at[1], zr_i.at[1])
    send(img(up, y).at[1], img(up, y).at[1], zs_i.at[3], zr_i.at[3], seq_0=down)
    z_half(0, 1, 0)
    z_half(1, 1, 1)
    z_half(1, 0, 0)
    z_half(0, 0, 1)
    z_half(1, 1, 0)
    z_half(0, 1, 1)
    y_first_small(1)
    y_first_small(2)
    core_in(0)
    attend(0)
    y_second_small(1)
    y_second_small(2)
    core_small(1)
    core_small(2)
    vacc[...] = grad_in(0)
    core_small_in(1)
    cross(1)
    grad_out(1)
    core_small_in(2)
    cross(2)
    grad_out(2)

    arrive(doc(far, y), zs_d.at[2], zr_d.at[2])
    arrive(img(far, y).at[0], zs_i.at[2], zr_i.at[2])
    arrive(img(far, y).at[1], zs_i.at[3], zr_i.at[3])
    y_first_small(3)
    owner_out(1)
    owner_out(2)
    y_second_small(3)
    core_small(3)
    core_small_in(3)
    cross(3)
    grad_out(3)

    z_half_in(0, 0, 0)
    z_half_in(0, 1, 0)
    send(item(down, y, 0), item(down, y, 0), zs_k.at[0, 4], zr_k.at[0, 4], seq_0=up)
    y_first(1, 0)
    z_half_in(1, 0, 1)
    z_half_in(1, 1, 1)
    send(item(up, y, 1), item(up, y, 1), zs_k.at[1, 4], zr_k.at[1, 4], seq_0=down)
    y_first(2, 1)
    owner_out(3)
    y_second(1, 0)
    y_second(2, 1)
    z_half_in(1, 0, 0)
    z_half_in(1, 1, 0)
    y_first(1, 1)
    z_half_in(0, 0, 1)
    z_half_in(0, 1, 1)
    y_first(2, 0)
    y_second(1, 1)
    core(1)
    y_second(2, 0)
    core(2)

    total = vacc[...]
    for r in (1, 2, 3):
        arrive(zr.at[r], rss.at[r], rsr.at[r])
    for r in (1, 2, 3):
        total += zr[r].astype(jnp.float32)
    vga[yc] = total.astype(jnp.bfloat16)
    for delta in range(1, 8):
        yy, cc = yc_of(delta)
        send(vga.at[yc], vga.at[yc], vss.at[delta], vsr.at[delta], seq_1=yy, seq_2=cc)
    core_in(1)
    pl.when(chunk[1] < h)(lambda: attend(1))

    for delta in range(1, 8):
        yy, cc = yc_of(8 - delta)
        arrive(gf.at[yy * 2 + cc], fss.at[delta], fsr.at[delta])
        arrive(vga.at[yy * 2 + cc], vss.at[delta], vsr.at[delta])
    term = lax.dot_general(
        gf[...].reshape(256, 256), vga[...].reshape(256, 256), (((0,), (0,)), ((), ())),
        preferred_element_type=jnp.float32,
    )
    fw[...] = jnp.concatenate(
        [term[:, :128].reshape(32, 8, 128), term[:, 128:].reshape(32, 8, 128)], axis=1
    ).astype(jnp.bfloat16)
    for delta in sorted(range(1, 32), key=lambda d: abs(d - 16)):
        hh, bb = z_of(delta)
        send(fw.at[bb * 4 + hh], fr.at[delta], wss.at[delta], wsr.at[delta], seq_0=hh, dp=bb)
    core_in(2)
    pl.when(chunk[2] < h)(lambda: attend(2))

    arrive(item(far, y, 0), zs_k.at[0, 4], zr_k.at[0, 4])
    y_first(3, 0)
    arrive(item(far, y, 1), zs_k.at[1, 4], zr_k.at[1, 4])
    y_first(3, 1)
    y_second(3, 0)
    y_second(3, 1)
    core(3)
    core_in(3)
    pl.when(chunk[3] < h)(lambda: attend(3))

    for g in range(2):
        out = (acc[g] / l_s[g] + xc[g]).astype(jnp.bfloat16)
        for i in range(4):
            out_ref[0, :, (g * 4 + i) * 128 : (g * 4 + i + 1) * 128] = out[i * 128 : (i + 1) * 128]

    whole = fw[b * 4 + h].astype(jnp.float32)
    for delta in range(1, 32):
        arrive(fr.at[delta], wss.at[delta], wsr.at[delta])
    for delta in range(1, 32):
        whole += fr[delta].astype(jnp.float32)
    wg_ref[:, :128] = whole[:5]
    wg_ref[:, 128:] = whole[8:13]
    for copy in sends:
        copy.wait_send()


def on_device(*args):
    bf, f32, i32 = jnp.bfloat16, jnp.float32, jnp.int32
    any_space = pl.BlockSpec(memory_space=pl.ANY)
    vmem = pl.BlockSpec(memory_space=pltpu.VMEM)
    V, D = pltpu.VMEM, pltpu.SemaphoreType.DMA
    pairs = [(3,), (4,), (2, 5), (4, 3), (4, 4), (4, 2, 3), (3, 4), (8,), (4, 8), (4,), (8,), (32,)]
    return pl.pallas_call(
        kernel,
        out_shape=(
            jax.ShapeDtypeStruct((1, 128, 1024), bf),
            jax.ShapeDtypeStruct((5, 256), f32),
        ),
        in_specs=[any_space] * 9 + [vmem] * 2,
        out_specs=(vmem, vmem),
        scratch_shapes=[
            V((128, 1024), bf), V((128, 1024), bf), V((128, 1024), bf), V((32, 1280), bf), V((1280, 256), bf),
            V((2, 4, 4, 2, 128, 256), bf), V((2, 4, 4, 2, 32, 256), bf), V((2, 4, 4, 1, 128), i32),
            V((8, 32, 256), bf), V((8, 32, 256), bf),
            V((4, 2, 4, 32, 256), bf), V((4, 8, 32, 256), bf),
            V((4, 32, 256), bf), V((4, 32, 256), bf),
            V((8, 32, 256), bf), V((32, 16, 128), bf), V((32, 16, 128), bf),
            V((2, 512, 128), f32), V((2, 512, 128), f32), V((2, 512, 128), f32), V((2, 512, 128), f32),
            V((128, 128), f32), V((128, 128), f32), V((128, 128), f32), V((32, 256), f32),
            D((9,)),
        ]
        + [D(shape) for shape in pairs for _ in (0, 1)],
        compiler_params=pltpu.CompilerParams(
            collective_id=0, has_side_effects=True, vmem_limit_bytes=48 * 1024 * 1024
        ),
    )(*args)


def solution(mesh):
    split = Mesh(
        mesh.devices.reshape(mesh.shape["dp"], 4, 4, 2, mesh.shape["tensor"]),
        ("dp", "seq_0", "seq_1", "seq_2", "tensor"),
    )
    placed = (
        P("dp", SEQ, "tensor"),
        P("dp", SEQ, "tensor"),
        P("dp", SEQ, "tensor"),
        P("dp", SEQ),
        P("dp", SEQ, "tensor"),
        P("dp", SEQ, "tensor"),
        P("dp", SEQ, "tensor"),
        P("dp", SEQ, None),
        P(None, "tensor"),
        P("dp", None),
        P("dp", None),
    )
    return jax.shard_map(
        on_device,
        mesh=split,
        in_specs=placed,
        out_specs=(P("dp", SEQ, "tensor"), P(DP_SEQ, "tensor")),
        check_vma=False,
    )
```

time: 469 us -> 124 us (0.26)
  waiting for transfers between devices: 226 us -> 0 us
  Pallas kernels: 0 us -> 112 us
  blocking collectives: 106 us -> 0 us
  matrix products: 38.2 us -> 0 us
  starting transfers between devices: 32.1 us -> 0 us
  local copies, waits for them, and re-layouts: 35.1 us -> 10.5 us
  between operations: 16.6 us -> 0.66 us
  other arithmetic: 13 us -> 0 us
    all_gather x5 -> x0, waiting for transfers between devices: 122 us -> none  [the longest x1 122 us: sent_together(): lax.all_gather(both, axis, axis=dim, tiled=True)]
    pallas_call x0 -> x1, Pallas kernels: none -> 112 us  [on_device(): pl.pallas_call(kernel, out_shape=(jax.ShapeDtypeStruct((1, 128, 1024), bf...]
    all_gather x5 -> x0, blocking collectives: 106 us -> none  [all_blocks(): blocks = lax.all_gather(blocks, axes[k], axis=0, tiled=True)]
    unnamed x7 -> x0, waiting for transfers between devices: 81.1 us -> none
    dot_general x21 -> x0, matrix products: 38.2 us -> none  [the longest x8 20.3 us: absorb_block(): jnp.einsum('gcts,sgd->gctd', weights.astype(jnp.bfloat16), value_heads, p...]
    all_to_all x2 -> x0, starting transfers between devices: 31.9 us -> none  [sent_and_summed(): lax.all_to_all(blocks, axis, split_axis=0, concat_axis=0, tiled=True)]
    all_to_all x2 -> x0, waiting for transfers between devices: 22.8 us -> none  [sent_and_summed(): lax.all_to_all(blocks, axis, split_axis=0, concat_axis=0, tiled=True)]
    dynamic_slice x32 -> x0, local copies, waits for them, and re-layouts: 16.6 us -> none  [absorb_all(): lax.scan(absorb_step, state_now, (key_blocks, value_blocks, doc_blocks, p...]
  transfers between devices with their start and end apart: 8 -> 0, of which waited for: 3 -> 0; matrix products, arithmetic and copies ran while one was open for 16% -> 0% of each run, Pallas kernels for 0% -> 0%
where the time goes in v1:
time: 124 us; the launch traced here: 123 us
  Pallas kernels  112 us (90%)
  local copies, waits for them, and re-layouts  10.5 us (8%)
    pallas_call x1, Pallas kernels, on_device(): pl.pallas_call(kernel, out_shape=(jax.ShapeDtypeStruct((1, 128, 1024), bf...  112 us
    unnamed x24, local copies, waits for them, and re-layouts  10.5 us

profile of v1, /device:TPU:1, one launch (start us, length us, event | category | flops | bytes accessed | tf_op | source)
XLA Modules:
  0.0 123.3 jit_solution(3607459782803798411)
XLA Ops:
  0.6 0.0 copy-start
  0.6 1.1 copy-done
  1.7 0.0 copy-start.1
  1.7 0.9 copy-done.1
  2.7 0.0 copy-start.2
  2.7 0.9 copy-done.2
  3.6 0.0 copy-start.3
  3.6 0.9 copy-done.3
  4.6 0.0 copy-start.4
  4.6 0.9 copy-done.4
  5.5 0.0 copy-start.5
  5.5 0.8 copy-done.5
  6.3 0.0 copy-start.6
  6.3 0.8 copy-done.6
  7.1 0.0 copy-start.7
  7.1 0.7 copy-done.7
  7.9 0.0 copy-start.8
  7.9 0.7 copy-done.8
  8.5 0.0 copy-start.9
  8.5 0.7 copy-done.9
  9.2 0.0 copy-start.10
  9.2 0.7 copy-done.10
  9.8 112.2 %shard_map.122 = (bf16[1,128,1024]{2,1,0:T(8,128)(2,1)S(1)}, f32[5,256]{1,0:T(8,128)S(1)}) custom-call(bf16[1,128,1024]{2,1,0:T(8,128)(2,1)S(1)} %copy-done.1, bf16[1,128,256]{2,1,0:T(8,128)(2,1)S(1)} %copy-done.5, bf16[1,128,256]{2,1,0:T(8,128)(2,1)S(1)} %copy-done.6, s32[1,128]{1,0:T(1,128)S(1)} %copy-done.8, bf16[1,128,1024]{2,1,0:T(8,128)(2,1)S(1)} %copy-done.2, ...), custom_call_target="tpu_custom_call" | custom-call | tf_op jit(solution)/shard_map/pallas_call | solution.py:433
  122.0 0.7 copy.15
  122.7 0.6 copy.16
Async XLA Ops:
  0.6 1.1 copy-start
  1.7 0.9 copy-start.1
  2.7 0.9 copy-start.2
  3.6 0.9 copy-start.3
  4.6 0.9 copy-start.4
  5.5 0.8 copy-start.5
  6.3 0.8 copy-start.6
  7.1 0.7 copy-start.7
  7.9 0.7 copy-start.8
  8.5 0.7 copy-start.9
  9.2 0.7 copy-start.10

commit v2 on v1

--- a/solution.py
+++ b/solution.py
@@ -43,20 +43,45 @@
     up, down, far = (h + 1) % 4, (h + 3) % 4, (h + 2) % 4
     right, left, across = (y + 1) % 4, (y + 3) % 4, (y + 2) % 4
     chunk = (h, down, up, far)
-    sends = []
-
-    def remote(src, dst, ss, rs, **where):
+    mate = 1 - c
+    conds = {
+        "all": None,
+        "up": h <= 2,
+        "low": h <= 1,
+        "first": h == 0,
+        "mid": (h == 1) | (h == 2),
+        "ends": (h == 0) | (h == 3),
+        1: h >= 1,
+        2: h == 3,
+        3: h >= 2,
+    }
+    sends = {key: [] for key in conds}
+    now = ["all"]
+
+    def on(key, *steps):
+        def run():
+            now[0] = key
+            for step in steps:
+                step()
+            now[0] = "all"
+
+        pl.when(conds[key])(run)
+
+    def at(ref, *index):
+        return ref, index
+
+    def remote(*parts, **where):
+        src, dst, ss, rs = (ref.at[index] for ref, index in parts)
         return pltpu.make_async_remote_copy(
             src_ref=src, dst_ref=dst, send_sem=ss, recv_sem=rs, device_id=where, device_id_type=MESH
         )
 
     def send(src, dst, ss, rs, **where):
-        copy = remote(src, dst, ss, rs, **where)
-        copy.start()
-        sends.append(copy)
+        remote(src, dst, ss, rs, **where).start()
+        sends[now[0]].append(lambda: remote(src, dst, ss, rs, **where))
 
     def arrive(dst, ss, rs):
-        remote(dst, dst, ss, rs, seq_2=1 - c).wait_recv()
+        remote(dst, dst, ss, rs, seq_2=mate).wait_recv()
 
     def yc_of(delta):
         other = (yc + delta) % 8
@@ -85,9 +110,10 @@
     rest = [fetch(q_hbm.at[0], q), fetch(qx_hbm.at[0], qx), fetch(ct_hbm.at[0], ct)]
 
     barrier = pltpu.get_barrier_semaphore()
-    for delta in (16, *range(1, 16), *range(17, 32)):
-        hh, bb = z_of(delta)
-        pl.semaphore_signal(barrier, inc=1, device_id={"seq_0": hh, "dp": bb}, device_id_type=MESH)
+    for where in (up, down):
+        pl.semaphore_signal(barrier, inc=1, device_id={"seq_0": where}, device_id_type=MESH)
+    for delta in range(1, 8):
+        pl.semaphore_signal(barrier, inc=1, device_id={"dp": (b + delta) % 8}, device_id_type=MESH)
     for delta in range(1, 8):
         yy, cc = yc_of(delta)
         pl.semaphore_signal(barrier, inc=1, device_id={"seq_1": yy, "seq_2": cc}, device_id_type=MESH)
@@ -125,84 +151,84 @@
     lo[...] = jnp.broadcast_to(image * IMG_TOK, (128, 128))
     hi[...] = jnp.broadcast_to(image * IMG_TOK + tile_count * TILE_TOK, (128, 128))
 
-    pl.semaphore_wait(barrier, 38)
+    pl.semaphore_wait(barrier, 16)
 
     def doc(hc, yy):
-        return dg.at[c, hc, yy]
-
-    def img(hc, yy):
-        return im.at[c, hc, yy]
+        return at(dg, c, hc, yy)
+
+    def img(hc, yy, *part):
+        return at(im, c, hc, yy, *part)
 
     def item(hc, yy, which):
-        return kv.at[c, hc, yy, which]
+        return at(kv, c, hc, yy, which)
 
     def half(hc, which, part):
-        return kv.at[c, hc, y, which, pl.ds(part * 64, 64)]
+        return at(kv, c, hc, y, which, pl.ds(part * 64, 64))
 
     def z_half(which, part, way):
         n = which * 2 + part
         where = up if way == 0 else down
-        send(half(h, which, part), half(h, which, part), zs_k.at[way, n], zr_k.at[way, n], seq_0=where)
+        send(half(h, which, part), half(h, which, part), at(zs_k, way, n), at(zr_k, way, n), seq_0=where)
 
     def z_half_in(which, part, way):
         n = which * 2 + part
         hc = down if way == 0 else up
-        arrive(half(hc, which, part), zs_k.at[way, n], zr_k.at[way, n])
+        arrive(half(hc, which, part), at(zs_k, way, n), at(zr_k, way, n))
 
     def y_first_small(r):
         hc = chunk[r]
         for way, where in ((0, right), (1, left)):
-            send(doc(hc, y), doc(hc, y), ys_d.at[r, way], yr_d.at[r, way], seq_1=where)
-            send(img(hc, y), img(hc, y), ys_i.at[r, way], yr_i.at[r, way], seq_1=where)
+            send(doc(hc, y), doc(hc, y), at(ys_d, r, way), at(yr_d, r, way), seq_1=where)
+            send(img(hc, y), img(hc, y), at(ys_i, r, way), at(yr_i, r, way), seq_1=where)
 
     def y_second_small(r):
         hc = chunk[r]
-        arrive(doc(hc, left), ys_d.at[r, 0], yr_d.at[r, 0])
-        send(doc(hc, left), doc(hc, left), ys_d.at[r, 2], yr_d.at[r, 2], seq_1=right)
-        arrive(img(hc, left), ys_i.at[r, 0], yr_i.at[r, 0])
-        send(img(hc, left).at[0], img(hc, left).at[0], ys_i.at[r, 2], yr_i.at[r, 2], seq_1=right)
-        arrive(doc(hc, right), ys_d.at[r, 1], yr_d.at[r, 1])
-        arrive(img(hc, right), ys_i.at[r, 1], yr_i.at[r, 1])
-        send(img(hc, right).at[1], img(hc, right).at[1], ys_i.at[r, 3], yr_i.at[r, 3], seq_1=left)
+        arrive(doc(hc, left), at(ys_d, r, 0), at(yr_d, r, 0))
+        send(doc(hc, left), doc(hc, left), at(ys_d, r, 2), at(yr_d, r, 2), seq_1=right)
+        arrive(img(hc, left), at(ys_i, r, 0), at(yr_i, r, 0))
+        send(img(hc, left, 0), img(hc, left, 0), at(ys_i, r, 2), at(yr_i, r, 2), seq_1=right)
+        arrive(doc(hc, right), at(ys_d, r, 1), at(yr_d, r, 1))
+        arrive(img(hc, right), at(ys_i, r, 1), at(yr_i, r, 1))
+        send(img(hc, right, 1), img(hc, right, 1), at(ys_i, r, 3), at(yr_i, r, 3), seq_1=left)
 
     def core_small(r):
         hc = chunk[r]
-        arrive(doc(hc, across), ys_d.at[r, 2], yr_d.at[r, 2])
-        send(dg.at[c, hc], dg.at[c, hc], cs.at[DOC, r], cr.at[DOC, r], seq_2=1 - c)
-        arrive(img(hc, across).at[0], ys_i.at[r, 2], yr_i.at[r, 2])
-        arrive(img(hc, across).at[1], ys_i.at[r, 3], yr_i.at[r, 3])
-        send(im.at[c, hc], im.at[c, hc], cs.at[KEY, r], cr.at[KEY, r], seq_2=1 - c)
+        arrive(doc(hc, across), at(ys_d, r, 2), at(yr_d, r, 2))
+        send(at(dg, c, hc), at(dg, c, hc), at(cs, DOC, r), at(cr, DOC, r), seq_2=mate)
+        arrive(img(hc, across, 0), at(ys_i, r, 2), at(yr_i, r, 2))
+        arrive(img(hc, across, 1), at(ys_i, r, 3), at(yr_i, r, 3))
+        send(at(im, c, hc), at(im, c, hc), at(cs, KEY, r), at(cr, KEY, r), seq_2=mate)
 
     def core_small_in(r):
         hc = chunk[r]
-        arrive(dg.at[1 - c, hc], cs.at[DOC, r], cr.at[DOC, r])
-        arrive(im.at[1 - c, hc], cs.at[KEY, r], cr.at[KEY, r])
+        arrive(at(dg, mate, hc), at(cs, DOC, r), at(cr, DOC, r))
+        arrive(at(im, mate, hc), at(cs, KEY, r), at(cr, KEY, r))
 
     def y_first(r, which):
         hc = chunk[r]
         for way, where in ((0, right), (1, left)):
-            send(item(hc, y, which), item(hc, y, which), ys_k.at[r, which, way], yr_k.at[r, which, way], seq_1=where)
+            send(item(hc, y, which), item(hc, y, which), at(ys_k, r, which, way), at(yr_k, r, which, way), seq_1=where)
 
     def y_second(r, which):
         hc = chunk[r]
         if which == 0:
-            arrive(item(hc, left, 0), ys_k.at[r, 0, 0], yr_k.at[r, 0, 0])
-            send(item(hc, left, 0), item(hc, left, 0), ys_k.at[r, 0, 2], yr_k.at[r, 0, 2], seq_1=right)
-            arrive(item(hc, right, 0), ys_k.at[r, 0, 1], yr_k.at[r, 0, 1])
+            arrive(item(hc, left, 0), at(ys_k, r, 0, 0), at(yr_k, r, 0, 0))
+            send(item(hc, left, 0), item(hc, left, 0), at(ys_k, r, 0, 2), at(yr_k, r, 0, 2), seq_1=right)
+            arrive(item(hc, right, 0), at(ys_k, r, 0, 1), at(yr_k, r, 0, 1))
         else:
-            arrive(item(hc, right, 1), ys_k.at[r, 1, 1], yr_k.at[r, 1, 1])
-            send(item(hc, right, 1), item(hc, right, 1), ys_k.at[r, 1, 2], yr_k.at[r, 1, 2], seq_1=left)
-            arrive(item(hc, left, 1), ys_k.at[r, 1, 0], yr_k.at[r, 1, 0])
+            arrive(item(hc, right, 1), at(ys_k, r, 1, 1), at(yr_k, r, 1, 1))
+            send(item(hc, right, 1), item(hc, right, 1), at(ys_k, r, 1, 2), at(yr_k, r, 1, 2), seq_1=left)
+            arrive(item(hc, left, 1), at(ys_k, r, 1, 0), at(yr_k, r, 1, 0))
 
     def core(r):
         hc = chunk[r]
-        arrive(item(hc, across, 0), ys_k.at[r, 0, 2], yr_k.at[r, 0, 2])
-        arrive(item(hc, across, 1), ys_k.at[r, 1, 2], yr_k.at[r, 1, 2])
-        send(kv.at[c, hc], kv.at[c, hc], cs.at[VAL, r], cr.at[VAL, r], seq_2=1 - c)
+        arrive(item(hc, across, 0), at(ys_k, r, 0, 2), at(yr_k, r, 0, 2))
+        arrive(item(hc, across, 1), at(ys_k, r, 1, 2), at(yr_k, r, 1, 2))
+        send(at(kv, c, hc), at(kv, c, hc), at(cs, VAL, r), at(cr, VAL, r), seq_2=mate)
 
     def core_in(r):
         hc = chunk[r]
-        arrive(kv.at[1 - c, hc], cs.at[VAL, r], cr.at[VAL, r])
+        arrive(at(kv, mate, hc), at(cs, VAL, r), at(cr, VAL, r))
 
     def stacked(ref, g):
         return jnp.concatenate(
@@ -269,29 +295,29 @@
     def grad_out(r):
         for delta in range(1, 8):
             yy, cc = yc_of(delta)
-            send(gs.at[r, cc, yy], gr.at[r, delta], gss.at[r, delta], gsr.at[r, delta], seq_1=yy, seq_2=cc)
+            send(at(gs, r, cc, yy), at(gr, r, delta), at(gss, r, delta), at(gsr, r, delta), seq_1=yy, seq_2=cc)
 
     def grad_in(r):
         total = gs[r, c, y].astype(jnp.float32)
         for delta in range(1, 8):
-            arrive(gr.at[r, delta], gss.at[r, delta], gsr.at[r, delta])
+            arrive(at(gr, r, delta), at(gss, r, delta), at(gsr, r, delta))
         for delta in range(1, 8):
             total += gr[r, delta].astype(jnp.float32)
         return total
 
     def owner_out(r):
         zs[r] = grad_in(r).astype(jnp.bfloat16)
-        send(zs.at[r], zr.at[r], rss.at[r], rsr.at[r], seq_0=chunk[r])
+        send(at(zs, r), at(zr, r), at(rss, r), at(rsr, r), seq_0=chunk[r])
 
     for way, where in ((0, up), (1, down)):
-        send(doc(h, y), doc(h, y), zs_d.at[way], zr_d.at[way], seq_0=where)
-        send(img(h, y), img(h, y), zs_i.at[way], zr_i.at[way], seq_0=where)
-    z_half(0, 0, 0)
-    z_half(1, 0, 1)
+        send(doc(h, y), doc(h, y), at(zs_d, way), at(zr_d, way), seq_0=where)
+        send(img(h, y), img(h, y), at(zs_i, way), at(zr_i, way), seq_0=where)
+    on("up", lambda: z_half(0, 0, 0))
+    on("low", lambda: z_half(1, 0, 1))
     y_first_small(0)
     for delta in range(1, 8):
         yy, cc = yc_of(delta)
-        send(fs.at[yy * 2 + cc], gf.at[yc], fss.at[delta], fsr.at[delta], seq_1=yy, seq_2=cc)
+        send(at(fs, yy * 2 + cc), at(gf, yc), at(fss, delta), at(fsr, delta), seq_1=yy, seq_2=cc)
     y_first(0, 0)
     y_first(0, 1)
     for copy in rest:
@@ -306,19 +332,16 @@
     grad_out(0)
     core(0)
 
-    arrive(doc(down, y), zs_d.at[0], zr_d.at[0])
-    send(doc(down, y), doc(down, y), zs_d.at[2], zr_d.at[2], seq_0=up)
-    arrive(img(down, y), zs_i.at[0], zr_i.at[0])
-    send(img(down, y).at[0], img(down, y).at[0], zs_i.at[2], zr_i.at[2], seq_0=up)
-    arrive(doc(up, y), zs_d.at[1], zr_d.at[1])
-    arrive(img(up, y), zs_i.at[1], zr_i.at[1])
-    send(img(up, y).at[1], img(up, y).at[1], zs_i.at[3], zr_i.at[3], seq_0=down)
-    z_half(0, 1, 0)
-    z_half(1, 1, 1)
-    z_half(1, 0, 0)
-    z_half(0, 0, 1)
-    z_half(1, 1, 0)
-    z_half(0, 1, 1)
+    arrive(doc(down, y), at(zs_d, 0), at(zr_d, 0))
+    send(doc(down, y), doc(down, y), at(zs_d, 2), at(zr_d, 2), seq_0=up)
+    arrive(img(down, y), at(zs_i, 0), at(zr_i, 0))
+    send(img(down, y, 0), img(down, y, 0), at(zs_i, 2), at(zr_i, 2), seq_0=up)
+    arrive(doc(up, y), at(zs_d, 1), at(zr_d, 1))
+    arrive(img(up, y), at(zs_i, 1), at(zr_i, 1))
+    send(img(up, y, 1), img(up, y, 1), at(zs_i, 3), at(zr_i, 3), seq_0=down)
+    on("up", lambda: z_half(0, 1, 0), lambda: z_half(1, 0, 0), lambda: z_half(1, 1, 0))
+    on("low", lambda: z_half(1, 1, 1))
+    on("first", lambda: z_half(0, 0, 1), lambda: z_half(0, 1, 1))
     y_first_small(1)
     y_first_small(2)
     core_in(0)
@@ -335,56 +358,66 @@
     cross(2)
     grad_out(2)
 
-    arrive(doc(far, y), zs_d.at[2], zr_d.at[2])
-    arrive(img(far, y).at[0], zs_i.at[2], zr_i.at[2])
-    arrive(img(far, y).at[1], zs_i.at[3], zr_i.at[3])
+    arrive(doc(far, y), at(zs_d, 2), at(zr_d, 2))
+    arrive(img(far, y, 0), at(zs_i, 2), at(zr_i, 2))
+    arrive(img(far, y, 1), at(zs_i, 3), at(zr_i, 3))
     y_first_small(3)
     owner_out(1)
     owner_out(2)
     y_second_small(3)
     core_small(3)
+
+    def keys_below():
+        z_half_in(0, 0, 0)
+        z_half_in(0, 1, 0)
+
+    def values_above():
+        z_half_in(1, 0, 1)
+        z_half_in(1, 1, 1)
+        send(item(up, y, 1), item(up, y, 1), at(zs_k, 1, 4), at(zr_k, 1, 4), seq_0=down)
+
+    on(1, keys_below)
+    on("mid", lambda: send(item(down, y, 0), item(down, y, 0), at(zs_k, 0, 4), at(zr_k, 0, 4), seq_0=up))
+    on(1, lambda: y_first(1, 0))
+    on("ends", values_above)
+    on(2, lambda: y_first(2, 1))
     core_small_in(3)
     cross(3)
     grad_out(3)
 
-    z_half_in(0, 0, 0)
-    z_half_in(0, 1, 0)
-    send(item(down, y, 0), item(down, y, 0), zs_k.at[0, 4], zr_k.at[0, 4], seq_0=up)
-    y_first(1, 0)
-    z_half_in(1, 0, 1)
-    z_half_in(1, 1, 1)
-    send(item(up, y, 1), item(up, y, 1), zs_k.at[1, 4], zr_k.at[1, 4], seq_0=down)
-    y_first(2, 1)
+    def keys_above():
+        z_half_in(0, 0, 1)
+        z_half_in(0, 1, 1)
+        y_first(2, 0)
+
+    def values_below():
+        z_half_in(1, 0, 0)
+        z_half_in(1, 1, 0)
+        y_first(1, 1)
+
+    on(1, lambda: y_second(1, 0))
+    on(2, lambda: y_second(2, 1), keys_above)
     owner_out(3)
-    y_second(1, 0)
-    y_second(2, 1)
-    z_half_in(1, 0, 0)
-    z_half_in(1, 1, 0)
-    y_first(1, 1)
-    z_half_in(0, 0, 1)
-    z_half_in(0, 1, 1)
-    y_first(2, 0)
-    y_second(1, 1)
-    core(1)
-    y_second(2, 0)
-    core(2)
+    on(1, values_below)
+    on(2, lambda: y_second(2, 0), lambda: core(2))
+    on(1, lambda: y_second(1, 1), lambda: core(1))
+    on(2, lambda: core_in(2), lambda: attend(2))
 
     total = vacc[...]
     for r in (1, 2, 3):
-        arrive(zr.at[r], rss.at[r], rsr.at[r])
+        arrive(at(zr, r), at(rss, r), at(rsr, r))
     for r in (1, 2, 3):
         total += zr[r].astype(jnp.float32)
     vga[yc] = total.astype(jnp.bfloat16)
     for delta in range(1, 8):
         yy, cc = yc_of(delta)
-        send(vga.at[yc], vga.at[yc], vss.at[delta], vsr.at[delta], seq_1=yy, seq_2=cc)
-    core_in(1)
-    pl.when(chunk[1] < h)(lambda: attend(1))
+        send(at(vga, yc), at(vga, yc), at(vss, delta), at(vsr, delta), seq_1=yy, seq_2=cc)
+    on(1, lambda: core_in(1), lambda: attend(1))
 
     for delta in range(1, 8):
         yy, cc = yc_of(8 - delta)
-        arrive(gf.at[yy * 2 + cc], fss.at[delta], fsr.at[delta])
-        arrive(vga.at[yy * 2 + cc], vss.at[delta], vsr.at[delta])
+        arrive(at(gf, yy * 2 + cc), at(fss, delta), at(fsr, delta))
+        arrive(at(vga, yy * 2 + cc), at(vss, delta), at(vsr, delta))
     term = lax.dot_general(
         gf[...].reshape(256, 256), vga[...].reshape(256, 256), (((0,), (0,)), ((), ())),
         preferred_element_type=jnp.float32,
@@ -394,19 +427,20 @@
     ).astype(jnp.bfloat16)
     for delta in sorted(range(1, 32), key=lambda d: abs(d - 16)):
         hh, bb = z_of(delta)
-        send(fw.at[bb * 4 + hh], fr.at[delta], wss.at[delta], wsr.at[delta], seq_0=hh, dp=bb)
-    core_in(2)
-    pl.when(chunk[2] < h)(lambda: attend(2))
-
-    arrive(item(far, y, 0), zs_k.at[0, 4], zr_k.at[0, 4])
-    y_first(3, 0)
-    arrive(item(far, y, 1), zs_k.at[1, 4], zr_k.at[1, 4])
-    y_first(3, 1)
-    y_second(3, 0)
-    y_second(3, 1)
-    core(3)
-    core_in(3)
-    pl.when(chunk[3] < h)(lambda: attend(3))
+        send(at(fw, bb * 4 + hh), at(fr, delta), at(wss, delta), at(wsr, delta), seq_0=hh, dp=bb)
+
+    def far_in():
+        arrive(item(far, y, 0), at(zs_k, 0, 4), at(zr_k, 0, 4))
+        y_first(3, 0)
+        arrive(item(far, y, 1), at(zs_k, 1, 4), at(zr_k, 1, 4))
+        y_first(3, 1)
+        y_second(3, 0)
+        y_second(3, 1)
+        core(3)
+        core_in(3)
+        attend(3)
+
+    on(3, far_in)
 
     for g in range(2):
         out = (acc[g] / l_s[g] + xc[g]).astype(jnp.bfloat16)
@@ -415,13 +449,21 @@
 
     whole = fw[b * 4 + h].astype(jnp.float32)
     for delta in range(1, 32):
-        arrive(fr.at[delta], wss.at[delta], wsr.at[delta])
+        arrive(at(fr, delta), at(wss, delta), at(wsr, delta))
     for delta in range(1, 32):
         whole += fr[delta].astype(jnp.float32)
     wg_ref[:, :128] = whole[:5]
     wg_ref[:, 128:] = whole[8:13]
-    for copy in sends:
-        copy.wait_send()
+
+    def drain(copies):
+        for copy in copies:
+            copy().wait_send()
+
+    for key, copies in sends.items():
+        if key == "all":
+            drain(copies)
+        elif copies:
+            pl.when(conds[key])(functools.partial(drain, copies))
 
 
 def on_device(*args):
@@ -451,7 +493,7 @@
         ]
         + [D(shape) for shape in pairs for _ in (0, 1)],
         compiler_params=pltpu.CompilerParams(
-            collective_id=0, has_side_effects=True, vmem_limit_bytes=48 * 1024 * 1024
+            collective_id=0, has_side_effects=True, vmem_limit_bytes=67043328
         ),
     )(*args)
 

time: 124 us -> 109 us (0.88)
  local copies, waits for them, and re-layouts: 10.5 us -> 2.28 us
  Pallas kernels: 112 us -> 106 us
    unnamed x24 -> x4, local copies, waits for them, and re-layouts: 10.5 us -> 2.28 us
    pallas_call x1, Pallas kernels: 112 us -> 106 us  [on_device(): pl.pallas_call(kernel, out_shape=(jax.ShapeDtypeStruct((1, 128, 1024), bf...]
where the time goes in v2:
time: 109 us
  Pallas kernels  106 us (97%)
  local copies, waits for them, and re-layouts  2.28 us (2%)
    pallas_call x1, Pallas kernels, on_device(): pl.pallas_call(kernel, out_shape=(jax.ShapeDtypeStruct((1, 128, 1024), bf...  106 us
    unnamed x4, local copies, waits for them, and re-layouts  2.28 us

profile of v2, /device:TPU:1, one launch (start us, length us, event | category | flops | bytes accessed | tf_op | source)
XLA Modules:
  0.0 108.5 jit_solution(552362246542124367)
XLA Ops:
  0.6 105.6 %shard_map.122 = (bf16[1,128,1024]{2,1,0:T(8,128)(2,1)}, f32[5,256]{1,0:T(8,128)}) custom-call(bf16[1,128,1024]{2,1,0:T(8,128)(2,1)} %q_hbm.1, bf16[1,128,256]{2,1,0:T(8,128)(2,1)} %k_hbm.1, bf16[1,128,256]{2,1,0:T(8,128)(2,1)} %v_hbm.1, s32[1,128]{1,0:T(1,128)} %docs_hbm.1, bf16[1,128,1024]{2,1,0:T(8,128)(2,1)} %qx_hbm.1, bf16[1,128,1024]{2,1,0:T(8,128)(2,1)} %ct_hbm.1, ...), custom_call_target="tpu_custom_call" | custom-call | tf_op jit(solution)/shard_map/pallas_call | solution.py:475
  106.3 0.0 copy-start
  106.3 1.7 %copy.15 = bf16[1,128,1024]{2,1,0:T(8,128)(2,1)} copy(bf16[1,128,1024]{2,1,0:T(8,128)(2,1)} %get-tuple-element.4) | data formatting | bytes 524288
  107.9 0.0 copy-done
  107.9 0.6 copy.16
Async XLA Ops:
  106.3 1.7 %copy-start = (f32[5,256]{1,0:T(8,128)S(1)}, f32[5,256]{1,0:T(8,128)}, u32[]{:S(2)}) copy-start(f32[5,256]{1,0:T(8,128)} %get-tuple-element.5) | copy-start | bytes 15364

commit v3 on v2

--- a/solution.py
+++ b/solution.py
@@ -49,6 +49,7 @@
         "up": h <= 2,
         "low": h <= 1,
         "first": h == 0,
+        "two": h == 2,
         "mid": (h == 1) | (h == 2),
         "ends": (h == 0) | (h == 3),
         1: h >= 1,
@@ -118,39 +119,8 @@
         yy, cc = yc_of(delta)
         pl.semaphore_signal(barrier, inc=1, device_id={"seq_1": yy, "seq_2": cc}, device_id_type=MESH)
 
-    got_f.wait()
-    got_w.wait()
-    im[c, h, y, 1] = jnp.dot(feat[...], w[...], preferred_element_type=jnp.float32).astype(jnp.bfloat16)
-
-    col = lax.broadcasted_iota(jnp.int32, (1, 256), 1)
-    wanted = jnp.where(col % 8 < 5, (col // 8) * 40 + col % 8, -1000)
-    vis_at = lax.broadcasted_iota(jnp.int32, (1280, 256), 0)
-
-    def pick(partner, _):
-        chosen = jnp.where(vis_at == wanted + partner * 5, 1.0, 0.0).astype(jnp.bfloat16)
-        fs[partner] = jnp.dot(feat[...], chosen, preferred_element_type=jnp.float32).astype(jnp.bfloat16)
-        return 0
-
-    lax.fori_loop(0, 8, pick, 0)
-    gf[yc] = fs[yc]
-
-    m_s[...] = jnp.full_like(m_s, NEG)
-    l_s[...] = jnp.zeros_like(l_s)
-    acc[...] = jnp.zeros_like(acc)
-    xc[...] = jnp.zeros_like(xc)
-
     for copy in first:
         copy.wait()
-    my_docs = jnp.broadcast_to(dg[c, h, y].astype(jnp.float32), (128, 128)).T
-    qd[...] = my_docs
-    number = lax.broadcasted_iota(jnp.int32, (128, 32), 1).astype(jnp.float32)
-    cites = jnp.broadcast_to(cite_ref[...].astype(jnp.float32), (128, 32))
-    counts = jnp.broadcast_to(tiles_ref[...].astype(jnp.float32), (128, 32))
-    image = jnp.sum(jnp.where(number == my_docs[:, :32], cites, 0.0), axis=1, keepdims=True)
-    tile_count = jnp.sum(jnp.where(number == image, counts, 0.0), axis=1, keepdims=True)
-    lo[...] = jnp.broadcast_to(image * IMG_TOK, (128, 128))
-    hi[...] = jnp.broadcast_to(image * IMG_TOK + tile_count * TILE_TOK, (128, 128))
-
     pl.semaphore_wait(barrier, 16)
 
     def doc(hc, yy):
@@ -311,15 +281,46 @@
 
     for way, where in ((0, up), (1, down)):
         send(doc(h, y), doc(h, y), at(zs_d, way), at(zr_d, way), seq_0=where)
-        send(img(h, y), img(h, y), at(zs_i, way), at(zr_i, way), seq_0=where)
-    on("up", lambda: z_half(0, 0, 0))
-    on("low", lambda: z_half(1, 0, 1))
+        send(img(h, y, 0), img(h, y, 0), at(zs_i, way), at(zr_i, way), seq_0=where)
+    got_f.wait()
+    got_w.wait()
+    im[c, h, y, 1] = jnp.dot(feat[...], w[...], preferred_element_type=jnp.float32).astype(jnp.bfloat16)
+    for way, where in ((0, up), (1, down)):
+        send(img(h, y, 1), img(h, y, 1), at(zs_i, 4 + way), at(zr_i, 4 + way), seq_0=where)
+    on("low", lambda: z_half(0, 0, 0), lambda: z_half(1, 0, 1))
     y_first_small(0)
+    y_first(0, 0)
+    y_first(0, 1)
+
+    col = lax.broadcasted_iota(jnp.int32, (1, 256), 1)
+    wanted = jnp.where(col % 8 < 5, (col // 8) * 40 + col % 8, -1000)
+    vis_at = lax.broadcasted_iota(jnp.int32, (1280, 256), 0)
+
+    def pick(partner, _):
+        chosen = jnp.where(vis_at == wanted + partner * 5, 1.0, 0.0).astype(jnp.bfloat16)
+        fs[partner] = jnp.dot(feat[...], chosen, preferred_element_type=jnp.float32).astype(jnp.bfloat16)
+        return 0
+
+    lax.fori_loop(0, 8, pick, 0)
+    gf[yc] = fs[yc]
+
     for delta in range(1, 8):
         yy, cc = yc_of(delta)
         send(at(fs, yy * 2 + cc), at(gf, yc), at(fss, delta), at(fsr, delta), seq_1=yy, seq_2=cc)
-    y_first(0, 0)
-    y_first(0, 1)
+    my_docs = jnp.broadcast_to(dg[c, h, y].astype(jnp.float32), (128, 128)).T
+    qd[...] = my_docs
+    number = lax.broadcasted_iota(jnp.int32, (128, 32), 1).astype(jnp.float32)
+    cites = jnp.broadcast_to(cite_ref[...].astype(jnp.float32), (128, 32))
+    counts = jnp.broadcast_to(tiles_ref[...].astype(jnp.float32), (128, 32))
+    image = jnp.sum(jnp.where(number == my_docs[:, :32], cites, 0.0), axis=1, keepdims=True)
+    tile_count = jnp.sum(jnp.where(number == image, counts, 0.0), axis=1, keepdims=True)
+    lo[...] = jnp.broadcast_to(image * IMG_TOK, (128, 128))
+    hi[...] = jnp.broadcast_to(image * IMG_TOK + tile_count * TILE_TOK, (128, 128))
+
+    m_s[...] = jnp.full_like(m_s, NEG)
+    l_s[...] = jnp.zeros_like(l_s)
+    acc[...] = jnp.zeros_like(acc)
+    xc[...] = jnp.zeros_like(xc)
     for copy in rest:
         copy.wait()
 
@@ -334,11 +335,14 @@
 
     arrive(doc(down, y), at(zs_d, 0), at(zr_d, 0))
     send(doc(down, y), doc(down, y), at(zs_d, 2), at(zr_d, 2), seq_0=up)
-    arrive(img(down, y), at(zs_i, 0), at(zr_i, 0))
+    arrive(img(down, y, 0), at(zs_i, 0), at(zr_i, 0))
     send(img(down, y, 0), img(down, y, 0), at(zs_i, 2), at(zr_i, 2), seq_0=up)
     arrive(doc(up, y), at(zs_d, 1), at(zr_d, 1))
-    arrive(img(up, y), at(zs_i, 1), at(zr_i, 1))
+    arrive(img(up, y, 0), at(zs_i, 1), at(zr_i, 1))
+    arrive(img(up, y, 1), at(zs_i, 5), at(zr_i, 5))
     send(img(up, y, 1), img(up, y, 1), at(zs_i, 3), at(zr_i, 3), seq_0=down)
+    arrive(img(down, y, 1), at(zs_i, 4), at(zr_i, 4))
+    on("two", lambda: z_half(0, 0, 0))
     on("up", lambda: z_half(0, 1, 0), lambda: z_half(1, 0, 0), lambda: z_half(1, 1, 0))
     on("low", lambda: z_half(1, 1, 1))
     on("first", lambda: z_half(0, 0, 1), lambda: z_half(0, 1, 1))
@@ -376,9 +380,12 @@
         z_half_in(1, 1, 1)
         send(item(up, y, 1), item(up, y, 1), at(zs_k, 1, 4), at(zr_k, 1, 4), seq_0=down)
 
-    on(1, keys_below)
-    on("mid", lambda: send(item(down, y, 0), item(down, y, 0), at(zs_k, 0, 4), at(zr_k, 0, 4), seq_0=up))
-    on(1, lambda: y_first(1, 0))
+    on(
+        "mid",
+        keys_below,
+        lambda: send(item(down, y, 0), item(down, y, 0), at(zs_k, 0, 4), at(zr_k, 0, 4), seq_0=up),
+        lambda: y_first(1, 0),
+    )
     on("ends", values_above)
     on(2, lambda: y_first(2, 1))
     core_small_in(3)
@@ -395,13 +402,11 @@
         z_half_in(1, 1, 0)
         y_first(1, 1)
 
-    on(1, lambda: y_second(1, 0))
-    on(2, lambda: y_second(2, 1), keys_above)
+    on("mid", lambda: y_second(1, 0))
+    on(2, lambda: y_second(2, 1))
     owner_out(3)
-    on(1, values_below)
-    on(2, lambda: y_second(2, 0), lambda: core(2))
-    on(1, lambda: y_second(1, 1), lambda: core(1))
-    on(2, lambda: core_in(2), lambda: attend(2))
+    on(2, keys_above, lambda: y_second(2, 0), lambda: core(2), keys_below, lambda: y_first(1, 0), lambda: y_second(1, 0))
+    on(1, values_below, lambda: y_second(1, 1), lambda: core(1))
 
     total = vacc[...]
     for r in (1, 2, 3):
@@ -412,7 +417,7 @@
     for delta in range(1, 8):
         yy, cc = yc_of(delta)
         send(at(vga, yc), at(vga, yc), at(vss, delta), at(vsr, delta), seq_1=yy, seq_2=cc)
-    on(1, lambda: core_in(1), lambda: attend(1))
+    on(2, lambda: core_in(2), lambda: attend(2))
 
     for delta in range(1, 8):
         yy, cc = yc_of(8 - delta)
@@ -428,6 +433,7 @@
     for delta in sorted(range(1, 32), key=lambda d: abs(d - 16)):
         hh, bb = z_of(delta)
         send(at(fw, bb * 4 + hh), at(fr, delta), at(wss, delta), at(wsr, delta), seq_0=hh, dp=bb)
+    on(1, lambda: core_in(1), lambda: attend(1))
 
     def far_in():
         arrive(item(far, y, 0), at(zs_k, 0, 4), at(zr_k, 0, 4))
@@ -471,7 +477,7 @@
     any_space = pl.BlockSpec(memory_space=pl.ANY)
     vmem = pl.BlockSpec(memory_space=pltpu.VMEM)
     V, D = pltpu.VMEM, pltpu.SemaphoreType.DMA
-    pairs = [(3,), (4,), (2, 5), (4, 3), (4, 4), (4, 2, 3), (3, 4), (8,), (4, 8), (4,), (8,), (32,)]
+    pairs = [(3,), (6,), (2, 5), (4, 3), (4, 4), (4, 2, 3), (3, 4), (8,), (4, 8), (4,), (8,), (32,)]
     return pl.pallas_call(
         kernel,
         out_shape=(

time: 109 us -> 114 us (1.046)
  Pallas kernels: 106 us -> 110 us
    pallas_call x1, Pallas kernels: 106 us -> 110 us  [on_device(): pl.pallas_call(kernel, out_shape=(jax.ShapeDtypeStruct((1, 128, 1024), bf...]
where the time goes in v3:
time: 114 us; the launch traced here: 113 us
  Pallas kernels  110 us (96%)
  local copies, waits for them, and re-layouts  2.28 us (2%)
    pallas_call x1, Pallas kernels, on_device(): pl.pallas_call(kernel, out_shape=(jax.ShapeDtypeStruct((1, 128, 1024), bf...  110 us

profile of v3, /device:TPU:1, one launch (start us, length us, event | category | flops | bytes accessed | tf_op | source)
XLA Modules:
  0.0 113.4 jit_solution(11610521409863033860)
XLA Ops:
  0.6 110.4 %shard_map.122 = (bf16[1,128,1024]{2,1,0:T(8,128)(2,1)}, f32[5,256]{1,0:T(8,128)}) custom-call(bf16[1,128,1024]{2,1,0:T(8,128)(2,1)} %q_hbm.1, bf16[1,128,256]{2,1,0:T(8,128)(2,1)} %k_hbm.1, bf16[1,128,256]{2,1,0:T(8,128)(2,1)} %v_hbm.1, s32[1,128]{1,0:T(1,128)} %docs_hbm.1, bf16[1,128,1024]{2,1,0:T(8,128)(2,1)} %qx_hbm.1, bf16[1,128,1024]{2,1,0:T(8,128)(2,1)} %ct_hbm.1, ...), custom_call_target="tpu_custom_call" | custom-call | tf_op jit(solution)/shard_map/pallas_call | solution.py:481
  111.1 0.0 copy-start
  111.1 1.7 %copy.15 = bf16[1,128,1024]{2,1,0:T(8,128)(2,1)} copy(bf16[1,128,1024]{2,1,0:T(8,128)(2,1)} %get-tuple-element.4) | data formatting | bytes 524288
  112.8 0.0 copy-done
  112.8 0.6 copy.16
Async XLA Ops:
  111.1 1.7 %copy-start = (f32[5,256]{1,0:T(8,128)S(1)}, f32[5,256]{1,0:T(8,128)}, u32[]{:S(2)}) copy-start(f32[5,256]{1,0:T(8,128)} %get-tuple-element.5) | copy-start | bytes 15364

commit v4 on v2

--- a/solution.py
+++ b/solution.py
@@ -396,12 +396,9 @@
         y_first(1, 1)
 
     on(1, lambda: y_second(1, 0))
-    on(2, lambda: y_second(2, 1), keys_above)
+    on(2, lambda: y_second(2, 1))
     owner_out(3)
     on(1, values_below)
-    on(2, lambda: y_second(2, 0), lambda: core(2))
-    on(1, lambda: y_second(1, 1), lambda: core(1))
-    on(2, lambda: core_in(2), lambda: attend(2))
 
     total = vacc[...]
     for r in (1, 2, 3):
@@ -412,7 +409,9 @@
     for delta in range(1, 8):
         yy, cc = yc_of(delta)
         send(at(vga, yc), at(vga, yc), at(vss, delta), at(vsr, delta), seq_1=yy, seq_2=cc)
-    on(1, lambda: core_in(1), lambda: attend(1))
+    on(2, keys_above)
+    on(1, lambda: y_second(1, 1), lambda: core(1))
+    on(2, lambda: y_second(2, 0), lambda: core(2))
 
     for delta in range(1, 8):
         yy, cc = yc_of(8 - delta)
@@ -428,6 +427,8 @@
     for delta in sorted(range(1, 32), key=lambda d: abs(d - 16)):
         hh, bb = z_of(delta)
         send(at(fw, bb * 4 + hh), at(fr, delta), at(wss, delta), at(wsr, delta), seq_0=hh, dp=bb)
+    on(1, lambda: core_in(1), lambda: attend(1))
+    on(2, lambda: core_in(2), lambda: attend(2))
 
     def far_in():
         arrive(item(far, y, 0), at(zs_k, 0, 4), at(zr_k, 0, 4))

time: 109 us -> 109 us (level)
  no operation moved by 1% of the time
where the time goes in v4:
time: 109 us; the launch traced here: 108 us
  Pallas kernels  105 us (96%)
  local copies, waits for them, and re-layouts  2.28 us (2%)
    pallas_call x1, Pallas kernels, on_device(): pl.pallas_call(kernel, out_shape=(jax.ShapeDtypeStruct((1, 128, 1024), bf...  105 us
    unnamed x4, local copies, waits for them, and re-layouts  2.28 us

profile of v4, /device:TPU:1, one launch (start us, length us, event | category | flops | bytes accessed | tf_op | source)
XLA Modules:
  0.0 108.1 jit_solution(16640857982108555204)
XLA Ops:
  0.6 105.2 %shard_map.122 = (bf16[1,128,1024]{2,1,0:T(8,128)(2,1)}, f32[5,256]{1,0:T(8,128)}) custom-call(bf16[1,128,1024]{2,1,0:T(8,128)(2,1)} %q_hbm.1, bf16[1,128,256]{2,1,0:T(8,128)(2,1)} %k_hbm.1, bf16[1,128,256]{2,1,0:T(8,128)(2,1)} %v_hbm.1, s32[1,128]{1,0:T(1,128)} %docs_hbm.1, bf16[1,128,1024]{2,1,0:T(8,128)(2,1)} %qx_hbm.1, bf16[1,128,1024]{2,1,0:T(8,128)(2,1)} %ct_hbm.1, ...), custom_call_target="tpu_custom_call" | custom-call | tf_op jit(solution)/shard_map/pallas_call | solution.py:476
  105.8 0.0 copy-start
  105.8 1.7 %copy.15 = bf16[1,128,1024]{2,1,0:T(8,128)(2,1)} copy(bf16[1,128,1024]{2,1,0:T(8,128)(2,1)} %get-tuple-element.4) | data formatting | bytes 524288
  107.5 0.0 copy-done
  107.5 0.6 copy.16
Async XLA Ops:
  105.8 1.7 %copy-start = (f32[5,256]{1,0:T(8,128)S(1)}, f32[5,256]{1,0:T(8,128)}, u32[]{:S(2)}) copy-start(f32[5,256]{1,0:T(8,128)} %get-tuple-element.5) | copy-start | bytes 15364
